TPU v7x, 32 devices: a whole 2x2x4 slice. The times are simulated.
32 devices in a mesh: slab: 4 (over y, core), patch: 8 (over z, x).
Axes of the slice: x: 2, y: 2, z: 4, core: 2. Of those that a mesh axis runs over, the one named last changes fastest.
Arguments:
- coarse: float32 [5, 64, 128, 128], P(None, 'slab', 'patch'), may hold values from -1.2 to 7.7, as said below
- fine: float32 [5, 128, 32, 1024], P(None, ('slab', 'patch')), may hold values from -1.2 to 7.7, as said below
- columns: int32 [32, 2], replicated, may hold values from 0 to 5, as said below
- patch_ids: int32 [4, 32], P('slab'), may hold values from 0 to 31, each once within a row
Outputs:
- coarse_out: float32 [5, 64, 128, 128], P(None, 'slab', 'patch')
- fine_out: float32 [5, 128, 32, 1024], P(None, ('slab', 'patch'))
Inputs may be any that keep to these rules, and one draw needn't show every extreme that they name: `coarse`: conserved variables of states with density and pressure between 0.5 and 2 and velocity components between -0.6 and 1.4. `fine`: conserved variables of states with density and pressure between 0.5 and 2 and velocity components between -0.6 and 1.4. `columns`: 32 distinct pairs (gy, gz) with gy below 6 and gz below 6. `patch_ids`: each row is a permutation of the 32 patch numbers of a slab.
All inputs are finite; a program needn't handle non-finite values.
Results may differ from a plain program's by a relative error of at most 0.00005.
Values sent between devices are 32-bit elements; how exact they have to be, the bound alone decides.
No kernel may reach another device: no remote copies, remote signals or barrier semaphores. Data moves between devices by JAX's collectives and lax.ppermute only.
A program may use at most 320 MiB of HBM per device.

v0:
```python
import jax
import jax.numpy as jnp
from jax import lax
from jax.sharding import PartitionSpec as P

P_SIZE = 32
LX = 1
GY = 6
GZ = 6
PYZ = 32
H = 16
heat_ratio = 1.4
fine_rate = 0.1
coarse_rate = 0.05
highest = lax.Precision.HIGHEST


def padded(block, sides, width):
    for axis, dim in sides:
        count = lax.axis_size(axis)
        forward = [(i, i + 1) for i in range(count - 1)]
        backward = [(target, source) for source, target in forward]
        low = lax.ppermute(
            lax.slice_in_dim(block, block.shape[dim] - width, None, axis=dim), axis, forward
        )
        high = lax.ppermute(lax.slice_in_dim(block, 0, width, axis=dim), axis, backward)
        block = jnp.concatenate([low, block, high], axis=dim)
    return block


def euler_flux(fields, normal_axis):
    density = fields[0]
    momentum = fields[1:4]
    energy = fields[4]
    velocity = momentum / density
    pressure = (heat_ratio - 1.0) * (energy - 0.5 * jnp.sum(momentum * velocity, axis=0))
    normal_speed = velocity[normal_axis]
    components = [
        momentum[normal_axis],
        momentum[0] * normal_speed,
        momentum[1] * normal_speed,
        momentum[2] * normal_speed,
        (energy + pressure) * normal_speed,
    ]
    components[1 + normal_axis] = components[1 + normal_axis] + pressure
    signal = jnp.abs(normal_speed) + jnp.sqrt(heat_ratio * pressure / density)
    return (jnp.stack(components), signal)


def rusanov(left_side, right_side, normal_axis):
    left_flux, left_signal = euler_flux(left_side, normal_axis)
    right_flux, right_signal = euler_flux(right_side, normal_axis)
    return 0.5 * (left_flux + right_flux) - 0.5 * jnp.maximum(left_signal, right_signal) * (
        right_side - left_side
    )


def advance(fields, ghosts):
    x_low, x_high, z_low, z_high, y_low, y_high = ghosts
    patch_count = fields.shape[1]
    side_cells = fields.shape[2]
    lane_count = side_cells * side_cells
    cube_view = fields.reshape(5, patch_count, side_cells, side_cells, side_cells)
    along_x = jnp.concatenate(
        [
            x_low.reshape(5, patch_count, 1, lane_count),
            fields,
            x_high.reshape(5, patch_count, 1, lane_count),
        ],
        axis=2,
    )
    flux_x = rusanov(along_x[:, :, :-1], along_x[:, :, 1:], 0)
    lane_index = jnp.arange(lane_count, dtype=jnp.int32)
    y_place = lane_index % side_cells
    z_place = lane_index // side_cells
    z_beyond = jnp.where(
        z_place == side_cells - 1,
        jnp.tile(z_high, (1, 1, 1, side_cells)),
        jnp.roll(fields, -side_cells, axis=3),
    )
    z_upper_flux = rusanov(fields, z_beyond, 2)
    z_edge = rusanov(z_low, cube_view[:, :, :, 0], 2)
    z_lower_flux = jnp.where(
        z_place == 0,
        jnp.tile(z_edge, (1, 1, 1, side_cells)),
        jnp.roll(z_upper_flux, side_cells, axis=3),
    )
    y_beyond = jnp.where(
        y_place == side_cells - 1,
        jnp.repeat(y_high, side_cells, axis=3),
        jnp.roll(fields, -1, axis=3),
    )
    y_upper_flux = rusanov(fields, y_beyond, 1)
    y_edge = rusanov(y_low, cube_view[..., 0], 1)
    y_lower_flux = jnp.where(
        y_place == 0, jnp.repeat(y_edge, side_cells, axis=3), jnp.roll(y_upper_flux, 1, axis=3)
    )
    change = (
        flux_x[:, :, 1:]
        - flux_x[:, :, :-1]
        + (z_upper_flux - z_lower_flux)
        + (y_upper_flux - y_lower_flux)
    )
    updated = fields - fine_rate * change
    y_top = y_upper_flux.reshape(5, patch_count, side_cells, side_cells, side_cells)[
        ..., side_cells - 1
    ]
    z_top = z_upper_flux[..., (side_cells - 1) * side_cells :]
    return (updated, (y_edge, y_top, z_edge, z_top))


def pair_mean(face_cells):
    extents = face_cells.shape
    return face_cells.reshape(extents[0], extents[1], extents[2] // 2, 2, extents[3] // 2, 2).mean(
        axis=(3, 5)
    )


def cell_mean(fields):
    extents = fields.shape
    return fields.reshape(
        extents[0], extents[1], extents[2] // 2, 2, extents[3] // 2, 2, extents[4] // 2, 2
    ).mean(axis=(3, 5, 7))


def upsample(face_cells):
    return jnp.repeat(jnp.repeat(face_cells, 2, axis=-2), 2, axis=-1)


def onehot(indices, extent):
    return (indices[:, None] == jnp.arange(extent, dtype=jnp.int32)[None, :]).astype(jnp.float32)


def neighbours(columns, step_y, step_z):
    matches = (columns[None, :, 0] == columns[:, None, 0] + step_y) & (
        columns[None, :, 1] == columns[:, None, 1] + step_z
    )
    present = jnp.any(matches, axis=1)
    partner = jnp.sum(
        jnp.where(matches, jnp.arange(columns.shape[0], dtype=jnp.int32)[None, :], 0), axis=1
    )
    return (present, partner)


def block_targets(column_y, column_z):
    grid_width = GY + 2
    return (
        (column_z + 1) * grid_width + column_y + 1,
        (column_z + 1) * grid_width + column_y,
        (column_z + 1) * grid_width + column_y + 2,
        column_z * grid_width + column_y + 1,
        (column_z + 2) * grid_width + column_y + 1,
    )


def cover_mask(columns):
    centre = block_targets(columns[:, 0], columns[:, 1])[0]
    occupied = jnp.sum(onehot(centre, (GZ + 2) * (GY + 2)), axis=0)
    return jnp.repeat(jnp.repeat(occupied.reshape(GZ + 2, GY + 2), H, axis=0), H, axis=1)


def block_form(slab):
    layer_depth = slab.shape[1] // H
    shaped = slab.reshape(5, layer_depth, H, GZ + 2, H, GY + 2, H).transpose(0, 1, 2, 4, 6, 3, 5)
    return shaped.reshape(5, layer_depth, H, H, H, (GZ + 2) * (GY + 2))


def slab_form(blocks):
    layer_depth = blocks.shape[1]
    shaped = blocks.reshape(5, layer_depth, H, H, H, GZ + 2, GY + 2).transpose(0, 1, 2, 5, 3, 6, 4)
    return shaped.reshape(5, layer_depth * H, (GZ + 2) * H, (GY + 2) * H)


def slot_order(numbers):
    slot_range = jnp.arange(numbers.shape[0], dtype=jnp.int32)
    found = jnp.sum(
        jnp.where(numbers[:, None] == slot_range[None, :], slot_range[:, None], 0), axis=0
    )
    return jnp.clip(found, 0, numbers.shape[0] - 1)


def coarse_faces(slab, layer_index, column_y, column_z):
    blocks = block_form(slab)
    layer_pick = onehot(layer_index, LX)
    centre, below_y, above_y, below_z, above_z = block_targets(column_y, column_z)
    nblocks = blocks.shape[-1]

    def select(portion, target):
        return jnp.einsum(
            "nl,nb,vlxzb->vnxz", layer_pick, onehot(target, nblocks), portion, precision=highest
        )

    return (
        select(blocks[:, :, :, :, H - 1], below_y),
        select(blocks[:, :, :, :, 0], above_y),
        select(blocks[:, :, :, H - 1], below_z),
        select(blocks[:, :, :, 0], above_z),
    )


def coarse_terms(averaged, face_terms, layer_index, column_y, column_z):
    layer_pick = onehot(layer_index, LX)
    centre, below_y, above_y, below_z, above_z = block_targets(column_y, column_z)
    nblocks = (GZ + 2) * (GY + 2)
    first_row = (jnp.arange(H) == 0).astype(jnp.float32)
    last_row = (jnp.arange(H) == H - 1).astype(jnp.float32)

    def spread(values, target):
        return jnp.einsum(
            "nl,nb,vnxz->vlxzb", layer_pick, onehot(target, nblocks), values, precision=highest
        )

    y_lower, y_upper, z_lower, z_upper = face_terms
    totals = jnp.einsum(
        "nl,nb,vnxzy->vlxzyb", layer_pick, onehot(centre, nblocks), averaged, precision=highest
    )
    totals = totals + spread(y_lower, below_y)[:, :, :, :, None, :] * last_row[:, None]
    totals = totals + spread(y_upper, above_y)[:, :, :, :, None, :] * first_row[:, None]
    totals = totals + spread(z_lower, below_z)[:, :, :, None, :, :] * last_row[:, None, None]
    totals = totals + spread(z_upper, above_z)[:, :, :, None, :, :] * first_row[:, None, None]
    return slab_form(totals)


def local(coarse, fine, columns, patch_ids):
    own_count = fine.shape[1]
    row_count = coarse.shape[2]
    patch_rank = lax.axis_index("patch")
    slab_rank = lax.axis_index("slab")
    slab_total = lax.axis_size("slab")
    numbers = patch_ids[0]
    own_numbers = lax.dynamic_slice_in_dim(numbers, patch_rank * own_count, own_count)
    inverse = slot_order(numbers)
    cube_fields = fine.reshape(5, own_count, P_SIZE, P_SIZE, P_SIZE)
    own_faces = jnp.stack(
        [
            cube_fields[:, :, 0],
            cube_fields[:, :, P_SIZE - 1],
            cube_fields[:, :, :, 0],
            cube_fields[:, :, :, P_SIZE - 1],
            cube_fields[..., 0],
            cube_fields[..., P_SIZE - 1],
        ]
    )
    slab_faces = lax.all_gather(own_faces, "patch", axis=2, tiled=True)
    slab_faces = jnp.take(slab_faces, inverse, axis=2)
    edge_faces = jnp.stack([slab_faces[0, :, :PYZ], slab_faces[1, :, -PYZ:]])
    rim_faces = padded(edge_faces, (("slab", 0),), 1)
    lower_rim = rim_faces[0]
    upper_rim = rim_faces[3]
    lower_source = jnp.where(slab_rank == 0, slab_faces[0, :, :PYZ], lower_rim)
    upper_source = jnp.where(slab_rank == slab_total - 1, slab_faces[1, :, -PYZ:], upper_rim)
    x_lower_table = jnp.concatenate([lower_source, slab_faces[1, :, :-PYZ]], axis=1)
    x_upper_table = jnp.concatenate([slab_faces[0, :, PYZ:], upper_source], axis=1)
    layer_index = own_numbers // PYZ
    column_index = own_numbers % PYZ
    column_y = columns[column_index, 0]
    column_z = columns[column_index, 1]
    whole_slab = lax.all_gather(coarse, "patch", axis=2, tiled=True)
    injected = coarse_faces(whole_slab, layer_index, column_y, column_z)

    def blend_faces(face_id, step_y, step_z, coarse_face):
        present, partner = neighbours(columns, step_y, step_z)
        target = layer_index * PYZ + partner[column_index]
        neighbour_face = jnp.take(slab_faces[face_id], target, axis=1)
        keep_mask = present[column_index][None, :, None, None]
        return jnp.where(keep_mask, neighbour_face, upsample(coarse_face))

    ghosts = (
        jnp.take(x_lower_table, own_numbers, axis=1),
        jnp.take(x_upper_table, own_numbers, axis=1),
        blend_faces(3, 0, -1, injected[2]),
        blend_faces(2, 0, 1, injected[3]),
        blend_faces(5, -1, 0, injected[0]),
        blend_faces(4, 1, 0, injected[1]),
    )
    updated, boundary = advance(fine, ghosts)

    def absent_mask(step_y, step_z):
        gaps = 1.0 - neighbours(columns, step_y, step_z)[0].astype(jnp.float32)
        return gaps[column_index][None, :, None, None]

    y_lower = -coarse_rate * pair_mean(boundary[0]) * absent_mask(-1, 0)
    y_upper = coarse_rate * pair_mean(boundary[1]) * absent_mask(1, 0)
    z_lower = -coarse_rate * pair_mean(boundary[2]) * absent_mask(0, -1)
    z_upper = coarse_rate * pair_mean(boundary[3]) * absent_mask(0, 1)
    averaged = cell_mean(updated.reshape(5, own_count, P_SIZE, P_SIZE, P_SIZE))
    placed = coarse_terms(
        averaged, (y_lower, y_upper, z_lower, z_upper), layer_index, column_y, column_z
    )
    contrib = lax.psum_scatter(placed, "patch", scatter_dimension=2, tiled=True)
    margin_cells = padded(coarse, (("slab", 1), ("patch", 2)), 1)
    before_x = jnp.where(slab_rank == 0, coarse[:, :1], margin_cells[:, :1, 1:-1])
    after_x = jnp.where(slab_rank == slab_total - 1, coarse[:, -1:], margin_cells[:, -1:, 1:-1])
    along_x = jnp.concatenate([before_x, coarse, after_x], axis=1)
    before_z = jnp.where(patch_rank == 0, coarse[:, :, :1], margin_cells[:, 1:-1, :1])
    after_z = jnp.where(
        patch_rank == lax.axis_size("patch") - 1, coarse[:, :, -1:], margin_cells[:, 1:-1, -1:]
    )
    along_z = jnp.concatenate([before_z, coarse, after_z], axis=2)
    along_y = jnp.concatenate([coarse[..., :1], coarse, coarse[..., -1:]], axis=3)
    covered = cover_mask(columns)
    own_cover = lax.dynamic_slice_in_dim(covered, patch_rank * row_count, row_count, 0)
    cover_z = lax.dynamic_slice_in_dim(
        jnp.pad(covered, ((1, 1), (0, 0))), patch_rank * row_count, row_count + 2, 0
    )
    cover_y = jnp.pad(own_cover, ((0, 0), (1, 1)))
    flux_x = rusanov(along_x[:, :-1], along_x[:, 1:], 0) * (1.0 - own_cover)
    flux_z = rusanov(along_z[:, :, :-1], along_z[:, :, 1:], 2) * (
        (1.0 - cover_z[:-1]) * (1.0 - cover_z[1:])
    )
    flux_y = rusanov(along_y[..., :-1], along_y[..., 1:], 1) * (
        (1.0 - cover_y[:, :-1]) * (1.0 - cover_y[:, 1:])
    )
    change = (
        flux_x[:, 1:]
        - flux_x[:, :-1]
        + (flux_z[:, :, 1:] - flux_z[:, :, :-1])
        + (flux_y[..., 1:] - flux_y[..., :-1])
    )
    provisional = coarse - coarse_rate * change
    coarse_out = jnp.where(own_cover > 0, contrib, provisional + contrib)
    return (coarse_out, updated)


def solution(mesh):
    return jax.shard_map(
        local,
        mesh=mesh,
        in_specs=(
            P(None, "slab", "patch", None),
            P(None, ("slab", "patch"), None, None),
            P(),
            P("slab", None),
        ),
        out_specs=(P(None, "slab", "patch", None), P(None, ("slab", "patch"), None, None)),
        check_vma=False,
    )
```

profile of v0, /device:TPU:0, one launch (start us, length us, event | category | flops | bytes accessed | tf_op | source)
XLA Modules:
  0.0 1050.5 jit_solution(5317102842722173065)
XLA Ops:
  7.2 7.9 reshape.643
  16.3 3.8 fusion.238
  20.1 16.2 %fusion.237 = (f32[5,4,32,32,1]{4,3,2,1,0:T(8,128)}, f32[5,4,32,32,1]{4,3,2,1,0:T(8,128)}) fusion(f32[5,4,32,32,32]{4,3,2,1,0:T(8,128)} %reshape.643), kind=kLoop, calls=%fused_computation.640 | loop fusion | bytes 327680 | tf_op jit(solution)/shard_map/slice | solution.py:241
  36.3 6.7 copy.483
  43.0 7.5 copy.484
  68.3 9.4 slice_reduce_fusion
  77.7 6.1 slice.909
  94.6 4.8 copy.501
  127.0 145.6 %all-gather.3.cloned.1.call-done = f32[6,5,32,32,32]{4,3,1,2,0:T(8,128)} async-done(((f32[6,5,4,32,32]{4,3,1,2,0:T(8,128)}), f32[6,5,32,32,32]{4,3,1,2,0:T(8,128)}) %all-gather.3.cloned.1.call-update) | async-done | bytes 3932176 | tf_op jit(solution)/shard_map/all_gather | solution.py:244
  272.5 13.7 %gather_fusion.2 = f32[32,6,5,32,32]{4,3,2,1,0:T(8,128)} fusion(f32[6,5,32,32,32]{4,3,1,2,0:T(8,128)} %all-gather.3.cloned.1.call-done, s32[1024]{0:T(1024)S(1)} %pad_clamp_fusion.6), kind=kCustom, calls=%fused_computation.8 | custom fusion | bytes 7864448 | tf_op jit(solution)/shard_map/jit(_take)/gather | solution.py:245
  286.2 6.8 copy_bitcast_fusion.1
  303.7 8.2 select_bitcast_fusion.1
  341.5 18.0 %all-gather.5.cloned.1.call-done = f32[5,16,128,128]{3,2,1,0:T(8,128)} async-done(((f32[5,16,16,128]{3,2,1,0:T(8,128)}), f32[5,16,128,128]{3,2,1,0:T(8,128)}) %all-gather.5.cloned.1.call-update) | async-done | bytes 5242896 | tf_op jit(solution)/shard_map/all_gather | solution.py:258
  359.5 24.1 %reshape.646 = f32[5,1,16,8,16,8,16]{6,5,4,3,2,0,1:T(8,128)} reshape(f32[5,16,128,128]{3,2,1,0:T(8,128)} %all-gather.5.cloned.1.call-done) | data formatting | bytes 10485760 | tf_op jit(solution)/shard_map/reshape | solution.py:164
  383.6 29.2 %copy.537 = f32[5,1,16,8,16,8,16]{6,5,3,4,2,0,1:T(8,128)} copy(f32[5,1,16,8,16,8,16]{6,5,4,3,2,0,1:T(8,128)} %reshape.646) | data formatting | bytes 10485760 | tf_op jit(solution)/shard_map/reshape | solution.py:164
  412.8 56.7 %fusion.234 = (f32[5,1,16,16,1,64]{4,5,3,2,0,1:T(8,128)}, f32[5,1,16,16,1,64]{4,5,3,2,0,1:T(8,128)}) fusion(f32[5,1,16,16,16,64]{4,5,3,2,0,1:T(8,128)} %bitcast.634), kind=kLoop, calls=%fused_computation.637 | loop fusion | bytes 1310720 | tf_op jit(solution)/shard_map/slice | solution.py:194
  477.0 23.0 %copy.496 = f32[5,1,16,16,1,64]{5,3,2,0,4,1:T(8,128)S(1)} copy(f32[5,1,16,16,1,64]{4,5,3,2,0,1:T(8,128)} %get-tuple-element.54) | data formatting | bytes 655360
  500.1 4.7 convolution_bitcast_fusion.4
  515.4 4.7 tile.8
  520.0 9.0 tile.9
  529.0 22.6 %copy.495 = f32[5,1,16,16,1,64]{5,3,2,0,4,1:T(8,128)S(1)} copy(f32[5,1,16,16,1,64]{4,5,3,2,0,1:T(8,128)} %get-tuple-element.55) | data formatting | bytes 655360
  551.7 4.7 convolution_bitcast_fusion.5
  557.2 5.9 broadcast_in_dim.211
  563.1 9.3 reshape.657
  589.7 12.0 %constant_dynamic-update-slice_fusion.1 = (f32[5,4,33,1024]{3,2,1,0:T(8,128)}, f32[5,4,32,1024]{3,2,1,0:T(8,128)}, f32[5,4,32,1024]{3,2,1,0:T(8,128)}) fusion(f32[5,4,32,1024]{3,2,1,0:T(8,128)S(1)} %copy-done.2, f32[5,4,32,1024]{3,2,1,0:T(8,128)} %copy-done.6, f32[4,32,1024]{2,1,0:T(8,128)S(1)} %get-tuple-element.86, ...), kind=kLoop, calls=%fused_computation.344 | loop fusion | flops 6553599 | bytes 27262976
  601.7 8.1 reshape.663
  615.0 3.3 reduce_sum.257
  622.7 3.3 reduce_sum.256
  628.8 10.6 %slice.916 = f32[5,4,32,32,1]{4,3,2,1,0:T(8,128)} slice(f32[5,4,32,32,32]{4,3,2,1,0:T(8,128)} %reshape.663), slice={[0:5], [0:4], [0:32], [0:32], [31:32]} | slice | bytes 163840 | tf_op jit(solution)/shard_map/slice | solution.py:105
  639.4 27.1 %copy.504 = f32[5,4,32,32,1]{0,3,2,1,4:T(8,128)} copy(f32[5,4,32,32,1]{4,3,2,1,0:T(8,128)} %slice.916) | data formatting | bytes 163840
  666.5 3.3 reduce_sum.255
  689.8 4.7 tile.20
  694.5 9.1 tile.21
  703.6 5.8 broadcast_in_dim.216
  709.4 9.1 reshape.661
  718.5 4.0 multiply_bitcast_fusion
  722.5 4.7 fusion.5
  728.5 3.9 fusion.11
  732.4 34.2 %copy.452 = f32[5,4,32,1024]{0,3,2,1:T(8,128)} copy(f32[5,4,32,1024]{3,2,1,0:T(8,128)} %fusion.11) | data formatting | bytes 5242880 | tf_op jit(solution)/shard_map/sub | solution.py:104
  766.6 49.4 %reduce_sum.253 = f32[5,4,16,16,16]{0,4,3,2,1:T(8,128)} reduce(f32[5,4,16,2,16,2,16,2]{0,7,6,5,4,3,2,1:T(2,128)} %bitcast.120, f32[]{:T(128)} %constant.88.clone.1), dimensions={3,5,7}, to_apply=%region_19.21 | reduce | flops 573440 | bytes 2949124 | tf_op jit(solution)/shard_map/reduce_sum | solution.py:123
  816.0 9.3 copy.453
  827.1 23.2 %fusion.2 = f32[5,1,16,16,16,64]{5,4,3,2,0,1:T(8,128)} fusion(f32[16]{0:T(128)S(1)} %copy-done.77, f32[5,16,16,64]{3,2,1,0:T(8,128)S(1)} %copy-done.46, f32[16]{0:T(128)S(1)} %copy-done.78, f32[5,16,16,64]{3,2,1,0:T(8,128)S(1)} %copy-done.47, f32[5,16,16,64]{3,2,1,0:T(8,128)S(1)} %copy-done.48, f32[5,16,16,64]{3,2,1,0:T(8,128)S(1)} %copy-done.49, ...), kind=kOutput, calls=%fused_computation.33 | convolution fusion | flops 73400832 | bytes 6881440 | tf_op jit(solution)/shard_map/nl,nb,vnxzy->vlxzyb/dot_general | solution.py:214
  850.2 24.4 %copy.467 = f32[5,1,16,16,16,64]{4,5,3,2,0,1:T(8,128)} copy(f32[5,1,16,16,16,64]{5,4,3,2,0,1:T(8,128)} %fusion.2) | data formatting | bytes 10485760 | tf_op jit(solution)/shard_map/add | solution.py:220
  874.6 29.1 %copy.468 = f32[5,1,16,8,16,8,16]{6,5,4,3,2,0,1:T(8,128)} copy(f32[5,1,16,8,16,8,16]{6,5,3,4,2,0,1:T(8,128)} %bitcast.637) | data formatting | bytes 10485760 | tf_op jit(solution)/shard_map/transpose | solution.py:170
  903.7 26.5 %reshape.667 = f32[5,16,128,128]{3,2,1,0:T(8,128)} reshape(f32[5,1,16,8,16,8,16]{6,5,4,3,2,0,1:T(8,128)} %copy.468) | data formatting | bytes 10485760 | tf_op jit(solution)/shard_map/reshape | solution.py:171
  931.2 11.1 %collective-permute-start.2 = (f32[5,1,16,128]{3,2,1,0:T(8,128)S(1)}, f32[5,1,16,128]{3,2,1,0:T(8,128)S(1)}, u32[]{:S(2)}, u32[]{:S(2)}) collective-permute-start(f32[5,1,16,128]{3,2,1,0:T(8,128)S(1)} %get-tuple-element.142), channel_id=1, source_target_pairs={{0,8},{8,16},{16,24},{1,9},{9,17},{17,25},{2,10},{10,18},{18,26},{... | collective-permute-start | bytes 122888 | tf_op jit(solution)/shard_map/ppermute | solution.py:23
  952.8 4.3 collective-permute-done.5
  958.4 82.4 %reduce-scatter.2.cloned.1.call-done = f32[5,16,16,128]{3,2,1,0:T(8,128)} async-done(((f32[5,16,128,128]{3,2,1,0:T(8,128)}), f32[5,16,16,128]{3,2,1,0:T(8,128)}) %reduce-scatter.2.cloned.1.call-update) | async-done | bytes 655376 | tf_op jit(solution)/shard_map/reduce_scatter | solution.py:290
  (394 shorter events, 183.7 us)
Async XLA Ops:
  7.2 265.3 %all-gather.3.cloned.1.call-start = ((), (), s32[]{:S(2)}) async-start(), calls=%async_computation.1 | async-start | bytes 17694720 | tf_op jit(solution)/shard_map/all_gather | solution.py:244
  43.0 10.7 %copy-start.30 = (f32[5,4,32,32,1]{3,2,0,1,4:T(8,128)}, f32[5,4,32,32,1]{3,2,0,1,4:T(8,128)S(1)}, u32[]{:S(2)}) copy-start(f32[5,4,32,32,1]{3,2,0,1,4:T(8,128)S(1)} %copy.483) | copy-start | bytes 245764
  50.4 3.9 copy-start.42
  50.5 6.2 copy-start
  51.8 6.0 copy-start.1
  55.2 304.4 %all-gather.5.cloned.1.call-start = ((), (), s32[]{:S(2)}) async-start(), calls=%async_computation.2 | async-start | bytes 5898240 | tf_op jit(solution)/shard_map/all_gather | solution.py:258
  55.9 984.9 %reduce-scatter.2.cloned.1.call-start = ((), (), s32[]{:S(2)}) async-start(), calls=%async_computation.3 | async-start | bytes 5898240 | tf_op jit(solution)/shard_map/reduce_scatter | solution.py:290
  112.8 13.0 %copy-start.52 = (f32[1,4,32,1,32]{4,3,2,1,0:T(1,128)}, f32[1,4,32,1,32]{4,3,2,1,0:T(1,128)S(1)}, u32[]{:S(2)}) copy-start(f32[1,4,32,1,32]{4,3,2,1,0:T(1,128)S(1)} %get-tuple-element.70) | copy-start | bytes 49156
  120.2 4.1 copy-start.58
  121.2 165.0 %copy-start.56 = (f32[4,32,32]{2,1,0:T(8,128)}, f32[4,32,32]{2,1,0:T(8,128)S(1)}, u32[]{:S(2)}) copy-start(f32[4,32,32]{2,1,0:T(8,128)S(1)} %get-tuple-element.161) | copy-start | bytes 49156
  293.0 4.2 copy-start.35
  293.7 6.7 collective-permute-start
  295.1 8.5 collective-permute-start.1
  325.2 15.4 %copy-start.22 = (f32[5,4,1,1024]{3,2,1,0:T(1,128)}, f32[5,4,1,1024]{3,2,1,0:T(1,128)S(1)}, u32[]{:S(2)}) copy-start(f32[5,4,1,1024]{3,2,1,0:T(1,128)S(1)} %copy.387) | copy-start | bytes 245764
  469.5 3.8 copy-start.38
  500.1 5.4 copy-start.37
  500.1 5.4 copy-start.68
  511.4 3.8 copy-start.36
  511.4 3.8 copy-start.67
  529.0 22.7 %copy-start.63 = (s32[4]{0:T(128)S(1)}, s32[4]{0:T(128)}, u32[]{:S(2)}) copy-start(s32[4]{0:T(128)} %broadcast_add_fusion) | copy-start | bytes 52
  551.7 5.4 copy-start.64
  551.7 5.4 copy-start.66
  563.1 9.3 slice-start.1
  563.1 9.4 copy-start.15
  563.1 9.4 copy-start.70
  612.7 6.8 copy-start.28
  612.8 6.8 copy-start.74
  618.4 8.2 copy-start.73
  666.5 3.9 copy-start.72
  669.9 6.7 copy-start.71
  670.5 8.2 copy-start.60
  694.5 9.1 copy-start.40
  709.4 9.1 copy-start.20
  709.4 9.1 copy-start.23
  718.5 4.0 copy-start.5
  722.4 4.8 copy-start.8
  722.4 4.8 copy-start.9
  722.5 5.2 copy-start.17
  722.5 6.0 copy-start.18
  722.5 6.0 copy-start.29
  722.5 6.0 copy-start.41
  722.5 6.0 copy-start.61
  722.5 6.0 copy-start.62
  930.2 13.5 %copy-start.75 = (s32[32]{0:T(128)S(1)}, s32[32]{0:T(128)}, u32[]{:S(2)}) copy-start(s32[32]{0:T(128)} %get-tuple-element.168) | copy-start | bytes 388
  931.2 16.8 %collective-permute-start.2 = (f32[5,1,16,128]{3,2,1,0:T(8,128)S(1)}, f32[5,1,16,128]{3,2,1,0:T(8,128)S(1)}, u32[]{:S(2)}, u32[]{:S(2)}) collective-permute-start(f32[5,1,16,128]{3,2,1,0:T(8,128)S(1)} %get-tuple-element.142), channel_id=1, source_target_pairs={{0,8},{8,16},{16,24},{1,9},{9,17},{17,25},{2,10},{10,18},{18,26},{... | collective-permute-start | bytes 122888 | tf_op jit(solution)/shard_map/ppermute | solution.py:23
  942.3 5.8 collective-permute-start.3
  948.2 4.5 collective-permute-start.4
  950.7 6.3 collective-permute-start.5
  (42 other events, 78.2 us)
Sparse Core Ops, SparseCore 0:
  55.3 217.1 all-gather.2
  274.5 84.9 all-gather.4
  930.3 110.4 reduce-scatter.1
where the time goes:
time: 1060 us; the launch traced here: 1050 us
  local copies, waits for them, and re-layouts  561 us (53%)
  waiting for transfers between devices  253 us (24%)
  other arithmetic  155 us (15%)
  matrix products  47.3 us (4%)
  starting transfers between devices  19.4 us (2%)
  between operations  15.5 us (1%)
    all_gather x1, waiting for transfers between devices, local(): slab_faces = lax.all_gather(own_faces, 'patch', axis=2, tiled=True)  146 us
    unnamed x179, local copies, waits for them, and re-layouts  124 us
    reduce_scatter x1, waiting for transfers between devices, local(): contrib = lax.psum_scatter(placed, 'patch', scatter_dimension=2, tiled=True)  82.4 us
    slice x1, local copies, waits for them, and re-layouts, coarse_faces(): blocks[:, :, :, :, H - 1]  56.7 us
    reshape x2, local copies, waits for them, and re-layouts, block_form(): slab.reshape(5, layer_depth, H, GZ + 2, H, GY + 2, H)  53.2 us
    reduce_sum x1, other arithmetic, cell_mean(): return fields.reshape(extents[0], extents[1], extents[2] // 2, 2, extents...  49.4 us
    sub x1, local copies, waits for them, and re-layouts, advance(): updated = fields - fine_rate * change  34.2 us
    transpose x1, local copies, waits for them, and re-layouts, slab_form(): blocks.reshape(5, layer_depth, H, H, H, GZ + 2, GY + 2)  29.1 us
  transfers between devices with their start and end apart: 9, of which 5 were waited for; matrix products, arithmetic and copies ran while one was open for 13% of the time, Pallas kernels for 0%

commit v1 on v0

--- a/solution.py
+++ b/solution.py
@@ -241,7 +241,9 @@
             cube_fields[..., P_SIZE - 1],
         ]
     )
-    slab_faces = lax.all_gather(own_faces, "patch", axis=2, tiled=True)
+    slab_faces = jnp.concatenate(
+        lax.all_to_all(jnp.stack([own_faces] * lax.axis_size("patch")), "patch", 0, 0), axis=2
+    )
     slab_faces = jnp.take(slab_faces, inverse, axis=2)
     edge_faces = jnp.stack([slab_faces[0, :, :PYZ], slab_faces[1, :, -PYZ:]])
     rim_faces = padded(edge_faces, (("slab", 0),), 1)

time: 1060 us -> 1020 us (0.962)
  waiting for transfers between devices: 253 us -> 130 us
  local copies, waits for them, and re-layouts: 561 us -> 606 us
  starting transfers between devices: 19.4 us -> 46 us
    all_gather x1 -> x0, waiting for transfers between devices: 146 us -> none  [local(): slab_faces = lax.all_gather(own_faces, 'patch', axis=2, tiled=True)]
    all_to_all x0 -> x1, waiting for transfers between devices: none -> 42.2 us  [local(): lax.all_to_all(jnp.stack([own_faces] * lax.axis_size('patch')), 'patch',...]
    ppermute x3, starting transfers between devices: 15 us -> 34 us  [padded(): lax.ppermute(lax.slice_in_dim(block, block.shape[dim] - width, None, axis...]
    all_gather x1, waiting for transfers between devices: 18 us -> 0.01 us  [local(): whole_slab = lax.all_gather(coarse, 'patch', axis=2, tiled=True)]
    all_to_all x0 -> x2, local copies, waits for them, and re-layouts: none -> 15.2 us  [local(): lax.all_to_all(jnp.stack([own_faces] * lax.axis_size('patch')), 'patch',...]
    all_to_all x0 -> x1, other arithmetic: none -> 13 us  [local(): lax.all_to_all(jnp.stack([own_faces] * lax.axis_size('patch')), 'patch',...]
    unnamed x179 -> x212, local copies, waits for them, and re-layouts: 124 us -> 130 us
    unnamed x42 -> x43, other arithmetic: 26.1 us -> 26.2 us
  transfers between devices with their start and end apart: 9 -> 9, of which waited for: 5 -> 4; matrix products, arithmetic and copies ran while one was open for 13% -> 24% of each run, Pallas kernels for 0% -> 0%
where the time goes in v1:
time: 1020 us; the launch traced here: 1010 us
  local copies, waits for them, and re-layouts  606 us (59%)
  other arithmetic  163 us (16%)
  waiting for transfers between devices  130 us (13%)
  matrix products  47.2 us (5%)
  starting transfers between devices  46 us (5%)
  between operations  16 us (2%)
    unnamed x212, local copies, waits for them, and re-layouts  130 us
    reduce_scatter x1, waiting for transfers between devices, local(): contrib = lax.psum_scatter(placed, 'patch', scatter_dimension=2, tiled=True)  81.5 us
    slice x1, local copies, waits for them, and re-layouts, coarse_faces(): blocks[:, :, :, :, H - 1]  56.7 us
    reshape x2, local copies, waits for them, and re-layouts, block_form(): slab.reshape(5, layer_depth, H, GZ + 2, H, GY + 2, H)  53.2 us
    reduce_sum x1, other arithmetic, cell_mean(): return fields.reshape(extents[0], extents[1], extents[2] // 2, 2, extents...  49.4 us
    all_to_all x1, waiting for transfers between devices, local(): lax.all_to_all(jnp.stack([own_faces] * lax.axis_size('patch')), 'patch',...  42.2 us
    ppermute x3, starting transfers between devices, padded(): lax.ppermute(lax.slice_in_dim(block, block.shape[dim] - width, None, axis...  34 us
    sub x1, local copies, waits for them, and re-layouts, advance(): updated = fields - fine_rate * change  34 us
  transfers between devices with their start and end apart: 9, of which 4 were waited for; matrix products, arithmetic and copies ran while one was open for 24% of the time, Pallas kernels for 0%

profile of v1, /device:TPU:0, one launch (start us, length us, event | category | flops | bytes accessed | tf_op | source)
XLA Modules:
  0.0 1009.3 jit_solution(10271743467268553345)
XLA Ops:
  7.9 7.9 reshape.651
  20.1 16.7 %fusion.226 = (f32[5,4,32,32,1]{4,3,2,1,0:T(8,128)}, f32[5,4,32,32,1]{4,3,2,1,0:T(8,128)}) fusion(f32[5,4,32,32,32]{4,3,2,1,0:T(8,128)} %reshape.651), kind=kLoop, calls=%fused_computation.626 | loop fusion | bytes 327680 | tf_op jit(solution)/shard_map/slice | solution.py:241
  36.8 6.7 copy.464
  43.5 7.5 copy.454
  52.1 7.5 stack.37
  59.6 12.3 %reshape.870 = f32[8,1,122880]{2,1,0:T(1,128)} reshape(f32[8,6,5,4,32,32]{5,4,3,2,1,0:T(8,128)} %stack.37) | data formatting | bytes 7864320
  71.9 7.6 all-to-all-start
  89.5 9.1 fusion.224
  109.9 6.1 slice.909
  121.7 5.0 copy.459
  140.0 42.2 %all-to-all-done = f32[8,1,122880]{2,1,0:T(1,128)} async-done(((f32[8,1,122880]{2,1,0:T(1,128)}), f32[8,1,122880]{2,1,0:T(1,128)}, u32[]{:S(2)}, u32[]{:S(2)}) %all-to-all-start) | async-done | bytes 3932192 | tf_op jit(solution)/shard_map/all_to_all | solution.py:245
  182.7 13.0 %reduce.6 = f32[8,122880]{1,0:T(8,128)} reduce(f32[8,1,122880]{2,1,0:T(1,128)} %all-to-all-done, f32[]{:T(128)} %broadcast.1234), dimensions={1}, to_apply=%all_to_all.3.reduce_sub_computation | reduce | bytes 7864324 | tf_op jit(solution)/shard_map/all_to_all | solution.py:245
  195.6 12.6 %reshape.871 = f32[8,6,5,4,32,32]{5,4,3,2,1,0:T(8,128)} reshape(f32[8,122880]{1,0:T(8,128)} %reduce.6) | data formatting | bytes 7864320
  208.3 14.7 %copy.371 = f32[8,6,5,4,32,32]{5,4,3,0,2,1:T(8,128)} copy(f32[8,6,5,4,32,32]{5,4,3,2,1,0:T(8,128)} %reshape.871) | data formatting | bytes 7864320 | tf_op jit(solution)/shard_map/all_to_all | solution.py:245
  223.0 13.4 %gather_fusion.2 = f32[32,6,5,32,32]{4,3,2,1,0:T(8,128)} fusion(f32[6,5,32,32,32]{4,3,2,1,0:T(8,128)} %bitcast.569, s32[1024]{0:T(1024)S(1)} %get-tuple-element.192), kind=kCustom, calls=%fused_computation.8 | custom fusion | bytes 7864448 | tf_op jit(solution)/shard_map/jit(_take)/gather | solution.py:247
  236.4 7.0 select_bitcast_fusion
  254.0 7.2 select_bitcast_fusion.2
  301.4 24.0 %reshape.656 = f32[5,1,16,8,16,8,16]{6,5,4,3,2,0,1:T(8,128)} reshape(f32[5,16,128,128]{3,2,1,0:T(8,128)} %all-gather.2.cloned.1.call-done) | data formatting | bytes 10485760 | tf_op jit(solution)/shard_map/reshape | solution.py:164
  325.4 29.2 %copy.514 = f32[5,1,16,8,16,8,16]{6,5,3,4,2,0,1:T(8,128)} copy(f32[5,1,16,8,16,8,16]{6,5,4,3,2,0,1:T(8,128)} %reshape.656) | data formatting | bytes 10485760 | tf_op jit(solution)/shard_map/reshape | solution.py:164
  354.5 56.7 %fusion.222 = (f32[5,1,16,16,1,64]{4,5,3,2,0,1:T(8,128)}, f32[5,1,16,16,1,64]{4,5,3,2,0,1:T(8,128)}) fusion(f32[5,1,16,16,16,64]{4,5,3,2,0,1:T(8,128)} %bitcast.565), kind=kLoop, calls=%fused_computation.622 | loop fusion | bytes 1310720 | tf_op jit(solution)/shard_map/slice | solution.py:194
  419.5 23.0 %copy.480 = f32[5,1,16,16,1,64]{5,3,2,0,4,1:T(8,128)S(1)} copy(f32[5,1,16,16,1,64]{4,5,3,2,0,1:T(8,128)} %get-tuple-element.57) | data formatting | bytes 655360
  442.6 4.7 convolution_bitcast_fusion.4
  456.4 4.6 tile.8
  461.0 9.0 tile.9
  470.0 22.6 %copy.479 = f32[5,1,16,16,1,64]{5,3,2,0,4,1:T(8,128)S(1)} copy(f32[5,1,16,16,1,64]{4,5,3,2,0,1:T(8,128)} %get-tuple-element.58) | data formatting | bytes 655360
  492.7 4.7 convolution_bitcast_fusion.5
  498.2 5.8 broadcast_in_dim.211
  504.1 9.3 reshape.667
  530.7 11.9 %constant_dynamic-update-slice_fusion.1 = (f32[5,4,33,1024]{3,2,1,0:T(8,128)}, f32[5,4,32,1024]{3,2,1,0:T(8,128)}, f32[5,4,32,1024]{3,2,1,0:T(8,128)}) fusion(f32[5,4,32,1024]{3,2,1,0:T(8,128)S(1)} %copy-done.2, f32[5,4,32,1024]{3,2,1,0:T(8,128)} %copy-done.6, f32[4,32,1024]{2,1,0:T(8,128)S(1)} %get-tuple-element.89, ...), kind=kLoop, calls=%fused_computation.345 | loop fusion | flops 6553599 | bytes 27262976
  542.6 8.1 reshape.673
  569.7 10.6 %slice.916 = f32[5,4,32,32,1]{4,3,2,1,0:T(8,128)} slice(f32[5,4,32,32,32]{4,3,2,1,0:T(8,128)} %reshape.673), slice={[0:5], [0:4], [0:32], [0:32], [31:32]} | slice | bytes 163840 | tf_op jit(solution)/shard_map/slice | solution.py:105
  580.4 27.1 %copy.483 = f32[5,4,32,32,1]{0,3,2,1,4:T(8,128)} copy(f32[5,4,32,32,1]{4,3,2,1,0:T(8,128)} %slice.916) | data formatting | bytes 163840
  630.8 4.7 tile.20
  635.5 9.0 tile.21
  644.5 5.8 broadcast_in_dim.216
  650.3 9.1 reshape.671
  659.4 3.9 multiply_bitcast_fusion
  663.4 4.7 fusion.5
  673.3 34.0 %copy.431 = f32[5,4,32,1024]{0,3,2,1:T(8,128)} copy(f32[5,4,32,1024]{3,2,1,0:T(8,128)} %fusion.11) | data formatting | bytes 5242880 | tf_op jit(solution)/shard_map/sub | solution.py:104
  707.3 49.4 %reduce_sum.253 = f32[5,4,16,16,16]{0,4,3,2,1:T(8,128)} reduce(f32[5,4,16,2,16,2,16,2]{0,7,6,5,4,3,2,1:T(2,128)} %bitcast.106, f32[]{:T(128)} %constant.88.clone.1), dimensions={3,5,7}, to_apply=%region_19.21 | reduce | flops 573440 | bytes 2949124 | tf_op jit(solution)/shard_map/reduce_sum | solution.py:123
  756.7 9.3 copy.432
  767.8 23.2 %fusion.2 = f32[5,1,16,16,16,64]{5,4,3,2,0,1:T(8,128)} fusion(f32[16]{0:T(128)S(1)} %copy-done.94, f32[5,16,16,64]{3,2,1,0:T(8,128)S(1)} %copy-done.53, f32[16]{0:T(128)S(1)} %copy-done.95, f32[5,16,16,64]{3,2,1,0:T(8,128)S(1)} %copy-done.54, f32[5,16,16,64]{3,2,1,0:T(8,128)S(1)} %copy-done.55, f32[5,16,16,64]{3,2,1,0:T(8,128)S(1)} %copy-done.56, ...), kind=kOutput, calls=%fused_computation.33 | convolution fusion | flops 73400832 | bytes 6881440 | tf_op jit(solution)/shard_map/nl,nb,vnxzy->vlxzyb/dot_general | solution.py:214
  790.9 24.3 %copy.446 = f32[5,1,16,16,16,64]{4,5,3,2,0,1:T(8,128)} copy(f32[5,1,16,16,16,64]{5,4,3,2,0,1:T(8,128)} %fusion.2) | data formatting | bytes 10485760 | tf_op jit(solution)/shard_map/add | solution.py:220
  815.3 29.1 %copy.447 = f32[5,1,16,8,16,8,16]{6,5,4,3,2,0,1:T(8,128)} copy(f32[5,1,16,8,16,8,16]{6,5,3,4,2,0,1:T(8,128)} %bitcast.568) | data formatting | bytes 10485760 | tf_op jit(solution)/shard_map/transpose | solution.py:170
  844.4 26.5 %reshape.677 = f32[5,16,128,128]{3,2,1,0:T(8,128)} reshape(f32[5,1,16,8,16,8,16]{6,5,4,3,2,0,1:T(8,128)} %copy.447) | data formatting | bytes 10485760 | tf_op jit(solution)/shard_map/reshape | solution.py:171
  871.9 28.9 %collective-permute-start.2 = (f32[5,1,16,128]{3,2,1,0:T(8,128)S(1)}, f32[5,1,16,128]{3,2,1,0:T(8,128)S(1)}, u32[]{:S(2)}, u32[]{:S(2)}) collective-permute-start(f32[5,1,16,128]{3,2,1,0:T(8,128)S(1)} %get-tuple-element.145), channel_id=1, source_target_pairs={{0,8},{8,16},{16,24},{1,9},{9,17},{17,25},{2,10},{10,18},{18,26},{... | collective-permute-start | bytes 122888 | tf_op jit(solution)/shard_map/ppermute | solution.py:23
  912.2 4.3 collective-permute-done.5
  917.8 81.5 %reduce-scatter.2.cloned.1.call-done = f32[5,16,16,128]{3,2,1,0:T(8,128)} async-done(((f32[5,16,128,128]{3,2,1,0:T(8,128)}), f32[5,16,16,128]{3,2,1,0:T(8,128)}) %reduce-scatter.2.cloned.1.call-update) | async-done | bytes 655376 | tf_op jit(solution)/shard_map/reduce_scatter | solution.py:292
  (440 shorter events, 197.6 us)
Async XLA Ops:
  7.2 294.2 %all-gather.2.cloned.1.call-start = ((), (), s32[]{:S(2)}) async-start(), calls=%async_computation.2 | async-start | bytes 5898240 | tf_op jit(solution)/shard_map/all_gather | solution.py:260
  20.1 30.9 %copy-start.33 = (f32[5,4,32,1,32]{4,3,2,1,0:T(1,128)}, f32[5,4,32,1,32]{4,3,2,1,0:T(1,128)S(1)}, u32[]{:S(2)}) copy-start(f32[5,4,32,1,32]{4,3,2,1,0:T(1,128)S(1)} %get-tuple-element.80) | copy-start | bytes 245764
  43.5 7.6 copy-start.37
  71.9 8.7 copy-start
  71.9 9.3 copy-start.81
  71.9 110.3 %all-to-all-start = ((f32[8,1,122880]{2,1,0:T(1,128)}), f32[8,1,122880]{2,1,0:T(1,128)}, u32[]{:S(2)}, u32[]{:S(2)}) async-start(f32[8,1,122880]{2,1,0:T(1,128)} %reshape.870), calls=%async_computation | async-start | bytes 7864320 | tf_op jit(solution)/shard_map/all_to_all | solution.py:245
  79.5 919.9 %reduce-scatter.2.cloned.1.call-start = ((), (), s32[]{:S(2)}) async-start(), calls=%async_computation.3 | async-start | bytes 5898240 | tf_op jit(solution)/shard_map/reduce_scatter | solution.py:292
  88.5 44.7 %copy-start.59 = (f32[1,4,32,1,32]{4,3,2,1,0:T(1,128)}, f32[1,4,32,1,32]{4,3,2,1,0:T(1,128)S(1)}, u32[]{:S(2)}) copy-start(f32[1,4,32,1,32]{4,3,2,1,0:T(1,128)S(1)} %get-tuple-element.76) | copy-start | bytes 49156
  88.5 49.6 %copy-start.49 = (f32[1,4,32,1,32]{4,3,2,1,0:T(1,128)}, f32[1,4,32,1,32]{4,3,2,1,0:T(1,128)S(1)}, u32[]{:S(2)}) copy-start(f32[1,4,32,1,32]{4,3,2,1,0:T(1,128)S(1)} %get-tuple-element.72) | copy-start | bytes 49156
  89.5 11.0 %copy-start.1 = (f32[5,4,32,1024]{3,2,1,0:T(8,128)S(1)}, f32[5,4,32,1024]{3,2,1,0:T(8,128)}, u32[]{:S(2)}) copy-start(f32[5,4,32,1024]{3,2,1,0:T(8,128)} %param.7) | copy-start | bytes 7864324
  98.7 38.7 %copy-start.57 = (f32[4,32,32]{2,1,0:T(8,128)}, f32[4,32,32]{2,1,0:T(8,128)S(1)}, u32[]{:S(2)}) copy-start(f32[4,32,32]{2,1,0:T(8,128)S(1)} %get-tuple-element.69) | copy-start | bytes 49156
  121.7 14.6 %copy-start.61 = (f32[1,4,32,32,1]{3,2,1,4,0:T(8,128)}, f32[1,4,32,32,1]{3,2,1,4,0:T(8,128)S(1)}, u32[]{:S(2)}) copy-start(f32[1,4,32,32,1]{3,2,1,4,0:T(8,128)S(1)} %copy.482) | copy-start | bytes 49156
  130.3 9.7 copy-start.70
  136.4 59.3 %copy-start.63 = (f32[4,32,32]{2,1,0:T(8,128)}, f32[4,32,32]{2,1,0:T(8,128)S(1)}, u32[]{:S(2)}) copy-start(f32[4,32,32]{2,1,0:T(8,128)S(1)} %get-tuple-element.159) | copy-start | bytes 49156
  244.0 6.7 collective-permute-start
  245.7 8.3 collective-permute-start.1
  285.8 14.6 %copy-start.27 = (f32[5,4,1,1024]{3,2,1,0:T(1,128)}, f32[5,4,1,1024]{3,2,1,0:T(1,128)S(1)}, u32[]{:S(2)}) copy-start(f32[5,4,1,1024]{3,2,1,0:T(1,128)S(1)} %copy.374) | copy-start | bytes 245764
  354.5 56.7 %copy-start.69 = (f32[4]{0:T(128)S(1)}, f32[4]{0:T(128)}, u32[]{:S(2)}) copy-start(f32[4]{0:T(128)} %get-tuple-element.186) | copy-start | bytes 52
  354.5 56.7 %copy-start.72 = (s32[4]{0:T(128)S(1)}, s32[4]{0:T(128)}, u32[]{:S(2)}) copy-start(s32[4]{0:T(128)} %get-tuple-element.173) | copy-start | bytes 52
  419.5 23.1 %copy-start.71 = (s32[4]{0:T(128)S(1)}, s32[4]{0:T(128)}, u32[]{:S(2)}) copy-start(s32[4]{0:T(128)} %copy-done.70) | copy-start | bytes 52
  442.6 5.4 copy-start.42
  442.6 5.4 copy-start.79
  442.6 5.4 copy-start.84
  470.0 22.7 %copy-start.76 = (s32[4]{0:T(128)S(1)}, s32[4]{0:T(128)}, u32[]{:S(2)}) copy-start(s32[4]{0:T(128)} %broadcast_add_fusion) | copy-start | bytes 52
  492.7 5.4 copy-start.77
  492.7 5.4 copy-start.82
  504.1 9.3 slice-start.1
  504.1 9.3 copy-start.15
  504.1 9.4 copy-start.87
  553.7 6.8 copy-start.35
  553.7 6.8 copy-start.91
  559.3 8.2 copy-start.90
  610.8 6.7 copy-start.88
  611.5 8.2 copy-start.68
  635.5 9.0 copy-start.45
  650.3 9.1 copy-start.25
  650.3 9.1 copy-start.28
  663.4 5.2 copy-start.22
  663.4 6.0 copy-start.23
  663.4 6.0 copy-start.36
  663.4 6.0 copy-start.46
  663.4 6.0 copy-start.74
  663.4 6.0 copy-start.75
  870.8 31.3 %copy-start.92 = (s32[32]{0:T(128)S(1)}, s32[32]{0:T(128)}, u32[]{:S(2)}) copy-start(s32[32]{0:T(128)} %get-tuple-element.166) | copy-start | bytes 388
  871.9 34.7 %collective-permute-start.2 = (f32[5,1,16,128]{3,2,1,0:T(8,128)S(1)}, f32[5,1,16,128]{3,2,1,0:T(8,128)S(1)}, u32[]{:S(2)}, u32[]{:S(2)}) collective-permute-start(f32[5,1,16,128]{3,2,1,0:T(8,128)S(1)} %get-tuple-element.145), channel_id=1, source_target_pairs={{0,8},{8,16},{16,24},{1,9},{9,17},{17,25},{2,10},{10,18},{18,26},{... | collective-permute-start | bytes 122888 | tf_op jit(solution)/shard_map/ppermute | solution.py:23
  900.9 5.8 collective-permute-start.3
  906.8 5.4 collective-permute-start.4
  910.2 6.3 collective-permute-start.5
  (59 other events, 141.7 us)
Sparse Core Ops, SparseCore 0:
  10.0 102.6 all-gather.1
  871.0 128.3 reduce-scatter.1
